TPU v7x, 32 devices: a whole 2x2x4 slice. The times are simulated.
32 devices in a mesh: section: 4 (over x, core), fsdp: 8 (over z, y).
Axes of the slice: x: 2, y: 2, z: 4, core: 2. Of those that a mesh axis runs over, the one named last changes fastest.
Arguments:
- tokens: bfloat16 [4, 2, 1024, 8192], P('section', None, 'fsdp'), may hold values from -6 to 6
- queries: bfloat16 [4, 2, 1024, 4096], P('section', None, 'fsdp'), may hold values from -200 to 200
- gains: bfloat16 [4, 8192], P('section'), may hold values from 0.5 to 1.5
- key_weight: bfloat16 [4, 8192, 512], P('section', 'fsdp'), may hold values from -0.0625 to 0.0625
- value_weight: bfloat16 [4, 8192, 512], P('section', 'fsdp'), may hold values from -0.0625 to 0.0625
- lengths: int32 [2, 16], replicated, may hold values from 1 to 128, 1024 in all within a row
Outputs:
- attended: bfloat16 [4, 2, 1024, 4096], P('section', None, 'fsdp')
Inputs may be any that keep to these rules, and one draw needn't show every extreme that they name: `lengths`: each row sums to 1024; some document has exactly 128 tokens.
All inputs are finite; a program needn't handle non-finite values.
Results may differ from a plain program's by a relative error of at most 0.012.
The roundings to bfloat16 on the way count: a program that leaves them out, or rounds other values in their place, can miss the bound.
Values may be sent and summed in bfloat16 or wider, within the bound.
A program may use at most 128 MiB of HBM per device.

v0:
```python
import jax
import jax.numpy as jnp
from jax import lax
from jax.sharding import PartitionSpec as P

HEAD = 128


def passed_along(block, axis, distance):
    devices = range(lax.axis_size(axis))
    route = [(i - distance, i) for i in devices if i - distance in devices]
    return lax.ppermute(block, axis, route)


def rms_norm(hidden, gain_row):
    widened = hidden.astype(jnp.float32)
    inverse_rms = lax.rsqrt(jnp.mean(widened * widened, axis=-1, keepdims=True) + 1e-05)
    return (widened * inverse_rms * gain_row.astype(jnp.float32)).astype(jnp.bfloat16)


def document_ids(length_row, positions):
    bounds = jnp.cumsum(length_row)
    return jnp.sum((bounds[None, :] <= positions[:, None]).astype(jnp.int32), axis=1)


def block_attend(query_rows, key_rows, value_rows, query_pos, key_pos, query_doc, key_doc):
    query_count = query_rows.shape[0]
    key_count = key_rows.shape[0]
    kv_count = key_rows.shape[1] // HEAD
    group_count = query_rows.shape[1] // (kv_count * HEAD)
    query_heads = query_rows.reshape(query_count, kv_count, group_count, HEAD)
    key_heads = key_rows.reshape(key_count, kv_count, HEAD)
    value_heads = value_rows.reshape(key_count, kv_count, HEAD)
    scores = jnp.einsum(
        "tkgd,skd->kgts", query_heads, key_heads, preferred_element_type=jnp.float32
    ) * HEAD ** (-0.5)
    allowed = (
        (key_doc[None, :] == query_doc[:, None])
        & (key_pos[None, :] <= query_pos[:, None])
        & (key_pos[None, :] >= 0)
    )
    scores = jnp.where(allowed, scores, -1e30)
    maxima = jnp.max(scores, axis=-1, keepdims=True)
    exponent = jnp.where(allowed, jnp.exp(scores - maxima), 0.0)
    totals = jnp.sum(exponent, axis=-1, keepdims=True)
    softmax_rows = (exponent / totals).astype(jnp.bfloat16)
    mixed = jnp.einsum(
        "kgts,skd->tkgd", softmax_rows, value_heads, preferred_element_type=jnp.float32
    )
    return mixed.reshape(query_count, kv_count * group_count * HEAD).astype(jnp.bfloat16)


def body(tokens, queries, gains, key_weight, value_weight, lengths):
    slot_count = tokens.shape[1]
    tok_count = tokens.shape[2]
    key_width = key_weight.shape[2]
    normed = rms_norm(tokens[0], gains[0])
    flat_rows = normed.reshape(slot_count * tok_count, normed.shape[2])

    def add_rows(weight_piece):
        return jnp.dot(flat_rows, weight_piece, preferred_element_type=jnp.float32)

    key_sums = add_rows(lax.all_gather(key_weight[0], "fsdp", axis=0, tiled=True))
    value_sums = add_rows(lax.all_gather(value_weight[0], "fsdp", axis=0, tiled=True))
    own_keys = key_sums.astype(jnp.bfloat16).reshape(slot_count, tok_count, key_width)
    own_values = value_sums.astype(jnp.bfloat16).reshape(slot_count, tok_count, key_width)
    prior_keys, prior_values = passed_along((own_keys, own_values), "fsdp", 1)
    all_keys = jnp.concatenate([prior_keys, own_keys], axis=1)
    all_values = jnp.concatenate([prior_values, own_values], axis=1)
    fsdp_index = lax.axis_index("fsdp")
    query_pos = fsdp_index * tok_count + jnp.arange(tok_count, dtype=jnp.int32)
    key_pos = fsdp_index * tok_count - tok_count + jnp.arange(2 * tok_count, dtype=jnp.int32)
    outputs = []
    for slot_index in range(slot_count):
        outputs.append(
            block_attend(
                queries[0, slot_index],
                all_keys[slot_index],
                all_values[slot_index],
                query_pos,
                key_pos,
                document_ids(lengths[slot_index], query_pos),
                document_ids(lengths[slot_index], key_pos),
            )
        )
    return jnp.stack(outputs)[None]


def solution(mesh):
    return jax.shard_map(
        body,
        mesh=mesh,
        in_specs=(
            P("section", None, "fsdp", None),
            P("section", None, "fsdp", None),
            P("section", None),
            P("section", "fsdp", None),
            P("section", "fsdp", None),
            P(),
        ),
        out_specs=P("section", None, "fsdp", None),
        check_vma=False,
    )
```

profile of v0, /device:TPU:16, one launch (start us, length us, event | category | flops | bytes accessed | tf_op | source)
XLA Modules:
  0.0 306.4 jit_solution(15095037703620579153)
XLA Ops:
  6.5 0.0 all-gather.5.cloned.1.call-start
  6.5 0.7 all-gather.5.cloned.1.call-update
  7.3 0.0 all-gather.7.cloned.1.call-start
  7.3 0.7 all-gather.7.cloned.1.call-update
  8.0 0.8 convert_element_type.101
  8.8 0.8 slice_bitcast_fusion
  9.6 0.1 copy.32
  9.7 0.1 reduce.1
  9.8 0.1 copy.40
  9.9 0.1 reduce.2
  10.0 1.7 fusion.38
  11.7 0.7 copy.60
  12.4 0.7 copy.59
  13.1 0.0 copy-start
  13.1 0.1 convert_reduce_fusion.3
  13.2 0.1 convert_reduce_fusion.1
  13.3 3.3 %multiply_reduce_fusion = f32[2,128]{1,0:T(2,128)S(1)} fusion(bf16[1,2,128,8192]{3,2,1,0:T(8,128)(2,1)} %param.6), kind=kLoop, calls=%fused_computation.9 | loop fusion | flops 6291200 | bytes 4195328 | tf_op jit(solution)/shard_map/reduce_sum | solution.py:17
  16.6 0.0 copy-done
  16.6 3.1 %fusion.7 = bf16[256,8192]{1,0:T(8,128)(2,1)} fusion(f32[8192]{0:T(1024)S(1)} %bitcast.100, f32[256]{0:T(256)S(1)} %rsqrt_bitcast_fusion, bf16[1,2,128,8192]{3,2,1,0:T(8,128)(2,1)S(1)} %copy-done), kind=kLoop, calls=%fused_computation.8 | loop fusion | flops 8388608 | bytes 8422400 | tf_op jit(solution)/shard_map/convert_element_type | solution.py:18
  19.7 114.5 %all-gather.5.cloned.1.call-done = bf16[1,8192,512]{2,1,0:T(8,128)(2,1)} async-done(((bf16[1,1024,512]{2,1,0:T(8,128)(2,1)}), bf16[1,8192,512]{2,1,0:T(8,128)(2,1)}) %all-gather.5.cloned.1.call-update) | async-done | bytes 8388624 | tf_op jit(solution)/shard_map/all_gather | solution.py:64
  134.1 7.0 %fusion.20 = bf16[256,512]{1,0:T(8,128)(2,1)S(1)} fusion(bf16[256,8192]{1,0:T(8,128)(2,1)} %fusion.7, bf16[1,8192,512]{2,1,0:T(8,128)(2,1)} %all-gather.5.cloned.1.call-done), kind=kOutput, calls=%fused_computation.29 | convolution fusion | flops 2147614720 | bytes 12845056 | tf_op jit(solution)/shard_map/dot_general | solution.py:61
  141.1 2.5 collective-permute-start
  143.6 119.8 %all-gather.7.cloned.1.call-done = bf16[1,8192,512]{2,1,0:T(8,128)(2,1)} async-done(((bf16[1,1024,512]{2,1,0:T(8,128)(2,1)}), bf16[1,8192,512]{2,1,0:T(8,128)(2,1)}) %all-gather.7.cloned.1.call-update) | async-done | bytes 8388624 | tf_op jit(solution)/shard_map/all_gather | solution.py:63
  263.4 7.0 %fusion.23 = bf16[256,512]{1,0:T(8,128)(2,1)S(1)} fusion(bf16[256,8192]{1,0:T(8,128)(2,1)} %fusion.7, bf16[1,8192,512]{2,1,0:T(8,128)(2,1)} %all-gather.7.cloned.1.call-done), kind=kOutput, calls=%fused_computation.30 | convolution fusion | flops 2147614720 | bytes 12845056 | tf_op jit(solution)/shard_map/dot_general | solution.py:61
  270.4 0.2 copy.33
  270.6 2.5 collective-permute-start.1
  273.1 0.2 fusion.32
  273.3 0.0 collective-permute-done
  273.3 0.1 copy.39
  273.5 7.3 %collective-permute-done.1 = bf16[2,128,512]{1,2,0:T(8,128)(2,1)} collective-permute-done((bf16[2,128,512]{1,2,0:T(8,128)(2,1)S(1)}, bf16[2,128,512]{1,2,0:T(8,128)(2,1)}, u32[]{:S(2)}, u32[]{:S(2)}) %collective-permute-start.1) | collective-permute-done | bytes 262176 | tf_op jit(solution)/shard_map/ppermute | solution.py:12
  280.8 1.7 fusion.30
  282.5 3.6 %fusion.39 = (f32[4,8,128]{2,1,0:T(8,128)S(1)}, f32[4,8,128,256]{2,3,1,0:T(8,128)}) fusion(pred[128,256]{0,1:T(8,128)(4,1)S(1)} %get-tuple-element.16, bf16[256,4,128,1]{0,2,3,1:T(8,128)(2,1)S(1)} %bitcast.99, bf16[128,4,8,128]{0,3,2,1:T(8,128)(2,1)S(1)} %bitcast.90), kind=kOutput, calls=%fused_computation.60 | convolution fusion | flops 273678592 | bytes 5554176 | tf_op jit(solution)/shard_map/sub | solution.py:44
  286.1 2.7 fusion.18
  288.8 0.5 copy.46
  289.4 0.8 copy.31
  290.2 0.0 copy-start.1
  290.2 4.6 %fusion.40 = (f32[4,8,128]{2,1,0:T(8,128)S(1)}, f32[4,8,128,256]{2,3,1,0:T(8,128)}) fusion(pred[128,256]{0,1:T(8,128)(4,1)S(1)} %get-tuple-element.15, bf16[256,4,128,1]{0,2,3,1:T(8,128)(2,1)} %bitcast.98, bf16[128,4,8,128]{0,3,2,1:T(8,128)(2,1)S(1)} %bitcast.89), kind=kOutput, calls=%fused_computation.61 | convolution fusion | flops 273678592 | bytes 5554176 | tf_op jit(solution)/shard_map/sub | solution.py:44
  294.8 0.0 copy-done.1
  294.8 2.7 fusion.19
  297.5 0.5 copy.45
  298.0 1.5 maximum_bitcast_fusion
  (7 shorter events, 0.1 us)
Async XLA Ops:
  6.5 127.6 %all-gather.5.cloned.1.call-start = ((), (), s32[]{:S(2)}) async-start(), calls=%async_computation | async-start | bytes 9437184 | tf_op jit(solution)/shard_map/all_gather | solution.py:64
  7.3 256.2 %all-gather.7.cloned.1.call-start = ((), (), s32[]{:S(2)}) async-start(), calls=%async_computation.1 | async-start | bytes 9437184 | tf_op jit(solution)/shard_map/all_gather | solution.py:63
  13.1 3.5 %copy-start = (bf16[1,2,128,8192]{3,2,1,0:T(8,128)(2,1)S(1)}, bf16[1,2,128,8192]{3,2,1,0:T(8,128)(2,1)}, u32[]{:S(2)}) copy-start(bf16[1,2,128,8192]{3,2,1,0:T(8,128)(2,1)} %param.6) | copy-start | bytes 12582916
  141.1 132.2 %collective-permute-start = (bf16[2,128,512]{2,1,0:T(8,128)(2,1)S(1)}, bf16[2,128,512]{2,1,0:T(8,128)(2,1)S(1)}, u32[]{:S(2)}, u32[]{:S(2)}) collective-permute-start(bf16[2,128,512]{2,1,0:T(8,128)(2,1)S(1)} %bitcast.96), channel_id=1, source_target_pairs={{0,1},{1,2},{2,3},{3,4},{4,5},{5,6},{6,7},{8,9},{9,10},{10,11},{11... | collective-permute-start | bytes 786440 | tf_op jit(solution)/shard_map/ppermute | solution.py:12
  270.6 10.2 %collective-permute-start.1 = (bf16[2,128,512]{1,2,0:T(8,128)(2,1)S(1)}, bf16[2,128,512]{1,2,0:T(8,128)(2,1)}, u32[]{:S(2)}, u32[]{:S(2)}) collective-permute-start(bf16[2,128,512]{1,2,0:T(8,128)(2,1)S(1)} %copy.33), channel_id=1, source_target_pairs={{0,1},{1,2},{2,3},{3,4},{4,5},{5,6},{6,7},{8,9},{9,10},{10,11},{11... | collective-permute-start | bytes 786440 | tf_op jit(solution)/shard_map/ppermute | solution.py:12
  290.2 4.6 %copy-start.1 = (bf16[1,256,512]{1,2,0:T(8,128)(2,1)S(1)}, bf16[1,256,512]{1,2,0:T(8,128)(2,1)}, u32[]{:S(2)}) copy-start(bf16[1,256,512]{1,2,0:T(8,128)(2,1)} %copy.31) | copy-start | bytes 786436
Sparse Core Ops, SparseCore 0:
  9.5 124.6 all-gather.4
  136.3 127.1 all-gather.6
where the time goes:
time: 307 us; the launch traced here: 306 us
  waiting for transfers between devices  243 us (79%)
  matrix products  27.5 us (9%)
  between operations  13.6 us (4%)
  other arithmetic  11.1 us (4%)
  local copies, waits for them, and re-layouts  6.13 us (2%)
  starting transfers between devices  4.96 us (2%)
    all_gather x1, waiting for transfers between devices, body(): lax.all_gather(key_weight[0], 'fsdp', axis=0, tiled=True)  120 us
    all_gather x1, waiting for transfers between devices, body(): lax.all_gather(value_weight[0], 'fsdp', axis=0, tiled=True)  114 us
    dot_general x2, matrix products, add_rows(): return jnp.dot(flat_rows, weight_piece, preferred_element_type=jnp.float32)  14 us
    sub x2, matrix products, block_attend(): exponent = jnp.where(allowed, jnp.exp(scores - maxima), 0.0)  8.16 us
    ppermute x2, waiting for transfers between devices, passed_along(): return lax.ppermute(block, axis, route)  7.35 us
  transfers between devices with their start and end apart: 4, of which 3 were waited for; matrix products, arithmetic and copies ran while one was open for 9% of the time, Pallas kernels for 0%

commit v1 on v0

v1 whole, which is shorter than its diff:
```python
import functools

import jax
import jax.numpy as jnp
from jax import lax
from jax.experimental import pallas as pl
from jax.experimental.pallas import tpu as pltpu
from jax.sharding import PartitionSpec as P

HEAD = 128
AXIS = "fsdp"


def kernel(
    n,
    x_hbm, q_hbm, gain_ref, kw_hbm, vw_hbm, len_ref, o_hbm,
    x_v, q_v, o_v, wbuf, xs, sx, part_s, part_r, own_acc, kv, prior, start_s,
    lw_sem, lx_sem, lq_sem, lo_sem,
    ws_sem, wr_sem, ys_sem, yr_sem, xs_sem, xr_sem, ps_sem, pr_sem, ks_sem, kr_sem,
):
    slots, tok, depth = x_v.shape
    chunks, groups, _, rows, _ = wbuf.shape
    wide = 2 * rows
    total = slots * tok
    q_per_kv = q_v.shape[2] // (chunks * HEAD)
    me = lax.axis_index(AXIS)
    bit = me % 2
    cls = (me // 2) % 2
    grp = me // 4
    y_peer = me + 1 - 2 * bit
    z_peer = me + 2 - 4 * cls
    right = lax.rem(me + 1, n)
    left = lax.rem(me + n - 1, n)
    others = [lax.rem(grp + d, groups) for d in range(1, groups)]

    def dev(g):
        return g * 4 + cls * 2 + bit

    def load_w(c):
        cols = pl.ds(c * HEAD, HEAD)
        return [
            pltpu.make_async_copy(
                w.at[0, :, cols], wbuf.at[c, grp, bit, :, pl.ds(i * HEAD, HEAD)], lw_sem.at[c, i]
            )
            for i, w in enumerate((kw_hbm, vw_hbm))
        ]

    x_loads = [pltpu.make_async_copy(x_hbm.at[0, s], x_v.at[s], lx_sem.at[s]) for s in range(slots)]
    q_load = pltpu.make_async_copy(q_hbm.at[0], q_v, lq_sem)
    w_loads = [load_w(c) for c in range(chunks)]
    for copy in w_loads[0] + x_loads:
        copy.start()
    for c in range(1, chunks):
        for copy in w_loads[c]:
            copy.start()
    q_load.start()

    prior[...] = jnp.zeros_like(prior)

    barrier = pltpu.get_barrier_semaphore()
    peers = [y_peer, z_peer, right, left] + [dev(g) for g in others]
    for peer in peers:
        pl.semaphore_signal(barrier, inc=1, device_id={AXIS: peer}, device_id_type=pl.DeviceIdType.MESH)
    pl.semaphore_wait(barrier, len(peers))

    def remote(src, dst, send, recv, peer):
        return pltpu.make_async_remote_copy(
            src_ref=src, dst_ref=dst, send_sem=send, recv_sem=recv,
            device_id={AXIS: peer}, device_id_type=pl.DeviceIdType.MESH,
        )

    def w_copy(c, source_grp, index_grp, peer):
        block = wbuf.at[c, source_grp, bit]
        return remote(block, block, ws_sem.at[c, index_grp], wr_sem.at[c, source_grp], peer)

    def y_copy(c, g, side):
        block = wbuf.at[c, g, side]
        return remote(block, block, ys_sem.at[c, g], yr_sem.at[c, g], y_peer)

    def send_w(c):
        for copy in w_loads[c]:
            copy.wait()
        for g in others:
            w_copy(c, grp, g, dev(g)).start()
        y_copy(c, grp, bit).start()

    def x_copy(s, g):
        return remote(
            sx.at[g, pl.ds(s * tok, tok)], xs.at[g, pl.ds(total + s * tok, tok)],
            xs_sem.at[s, g], xr_sem.at[s, g], z_peer,
        )

    def p_copy(c):
        return remote(part_s.at[c], part_r.at[c], ps_sem.at[c], pr_sem.at[c], z_peer)

    def k_copy(c):
        return remote(kv.at[c], prior.at[c], ks_sem.at[c], kr_sem.at[c], right)

    send_w(0)

    block_rows = 16

    def norm_block(s, r):
        here = pl.ds(pl.multiple_of(r * block_rows, block_rows), block_rows)
        there = pl.ds(pl.multiple_of(s * tok + r * block_rows, block_rows), block_rows)
        squares = jnp.zeros((block_rows, 1), jnp.float32)
        step = 2 * wide
        for i in range(depth // step):
            piece = x_v[s, here, i * step:(i + 1) * step].astype(jnp.float32)
            squares = squares + jnp.sum(piece * piece, axis=-1, keepdims=True)
        inverse = lax.rsqrt(squares / depth + 1e-05)
        for g in range(groups):
            for mine in (True, False):
                first = (4 * g + 2 * (cls if mine else 1 - cls)) * rows
                cols = pl.ds(pl.multiple_of(first, HEAD), wide)
                value = x_v[s, here, cols].astype(jnp.float32) * inverse
                value = (value * gain_ref[0:1, cols].astype(jnp.float32)).astype(jnp.bfloat16)
                if mine:
                    xs[g, there, :] = value
                else:
                    sx[g, there, :] = value

    for s in range(slots):
        x_loads[s].wait()

        def norm_step(r, carry, s=s):
            norm_block(s, r)
            return carry

        lax.fori_loop(0, tok // block_rows, norm_step, 0)
        for g in range(groups):
            x_copy(s, g).start()

    for c in range(1, chunks):
        send_w(c)

    docs = len_ref.shape[1]
    rowi = lax.broadcasted_iota(jnp.int32, (docs, docs), 0)
    coli = lax.broadcasted_iota(jnp.int32, (docs, docs), 1)
    pos = lax.broadcasted_iota(jnp.int32, (tok, 1), 0) + me * tok
    for s in range(slots):
        lens = jnp.broadcast_to(len_ref[s:s + 1, :], (docs, docs))
        bounds = jnp.sum(jnp.where(coli <= rowi, lens, 0), axis=1, keepdims=True)
        bound_row = jnp.sum(jnp.where(coli == rowi, bounds, 0), axis=0, keepdims=True)
        start = jnp.max(jnp.where(bound_row <= pos, bound_row, 0), axis=1, keepdims=True)
        start_s[s] = jnp.broadcast_to(start, (tok, HEAD))
    q_load.wait()

    def forward(c):
        for g in others:
            w_copy(c, g, g, dev(g)).wait_recv()
            y_copy(c, g, bit).start()

    def project(c, lo):
        acc = jnp.zeros((total, 2 * HEAD), jnp.float32)
        for g in range(groups):
            acc = acc + jnp.dot(
                xs[g, lo:lo + total, :], wbuf[c, g].reshape(wide, 2 * HEAD),
                preferred_element_type=jnp.float32,
            )
        return acc

    def stage_a(c):
        for g in range(groups):
            y_copy(c, g, 1 - bit).wait_recv()
        if c == 0:
            for s in range(slots):
                for g in range(groups):
                    x_copy(s, g).wait_recv()
        part_s[c] = project(c, total)
        p_copy(c).start()
        own_acc[c] = project(c, 0)

    def stage_b(c):
        p_copy(c).wait_recv()
        kv[c] = (own_acc[c] + part_r[c]).astype(jnp.bfloat16)

        @pl.when(me < n - 1)
        def _():
            k_copy(c).start()

    key_pos = lax.broadcasted_iota(jnp.int32, (tok, 2 * tok), 1) + (me - 1) * tok
    query_pos = lax.broadcasted_iota(jnp.int32, (tok, 2 * tok), 0) + me * tok

    def out_copy(c):
        cols = pl.ds(c * q_per_kv * HEAD, q_per_kv * HEAD)
        return pltpu.make_async_copy(o_v.at[:, :, cols], o_hbm.at[0, :, :, cols], lo_sem.at[c])

    def stage_c(c):
        @pl.when(me > 0)
        def _():
            k_copy(c).wait_recv()

        for s in range(slots):
            here = slice(s * tok, (s + 1) * tok)
            keys = jnp.concatenate([prior[c, here, 0:HEAD], kv[c, here, 0:HEAD]], axis=0)
            values = jnp.concatenate([prior[c, here, HEAD:], kv[c, here, HEAD:]], axis=0)
            allowed = (key_pos >= start_s[s][:, 0:1]) & (key_pos <= query_pos)

            def head_step(h, carry, s=s, keys=keys, values=values, allowed=allowed):
                cols = pl.ds(pl.multiple_of((c * q_per_kv + h) * HEAD, HEAD), HEAD)
                scores = lax.dot_general(
                    q_v[s, :, cols], keys, (((1,), (1,)), ((), ())),
                    preferred_element_type=jnp.float32,
                ) * HEAD ** (-0.5)
                scores = jnp.where(allowed, scores, -1e30)
                maxima = jnp.max(scores, axis=-1, keepdims=True)
                exponent = jnp.where(allowed, jnp.exp(scores - maxima), 0.0)
                sums = jnp.sum(exponent, axis=-1, keepdims=True)
                soft = (exponent / sums).astype(jnp.bfloat16)
                mixed = jnp.dot(soft, values, preferred_element_type=jnp.float32)
                o_v[s, :, cols] = mixed.astype(jnp.bfloat16)
                return carry

            lax.fori_loop(0, q_per_kv, head_step, 0, unroll=2)
        out_copy(c).start()

    for step in range(chunks + 4):
        if step < chunks:
            forward(step)
        if 1 <= step <= chunks:
            stage_a(step - 1)
        if 2 <= step <= chunks + 1:
            stage_b(step - 2)
        if 3 <= step <= chunks + 2:
            stage_c(step - 3)

    for c in range(chunks):
        out_copy(c).wait()
        for g in others:
            w_copy(c, grp, g, dev(g)).wait_send()
        for g in range(groups):
            y_copy(c, g, bit).wait_send()
        p_copy(c).wait_send()

        @pl.when(me < n - 1)
        def _(c=c):
            k_copy(c).wait_send()

    for s in range(slots):
        for g in range(groups):
            x_copy(s, g).wait_send()


def body(tokens, queries, gains, key_weight, value_weight, lengths):
    n = lax.axis_size(AXIS)
    _, slots, tok, depth = tokens.shape
    _, rows, key_width = key_weight.shape
    chunks = key_width // HEAD
    groups = n // 4
    total = slots * tok
    bf, f32 = jnp.bfloat16, jnp.float32
    any_spec = pl.BlockSpec(memory_space=pl.ANY)
    vmem_spec = pl.BlockSpec(memory_space=pltpu.VMEM)
    dma = pltpu.SemaphoreType.DMA
    return pl.pallas_call(
        functools.partial(kernel, n),
        out_shape=jax.ShapeDtypeStruct(queries.shape, bf),
        in_specs=[any_spec, any_spec, vmem_spec, any_spec, any_spec, vmem_spec],
        out_specs=any_spec,
        scratch_shapes=[
            pltpu.VMEM((slots, tok, depth), bf),
            pltpu.VMEM(queries.shape[1:], bf),
            pltpu.VMEM(queries.shape[1:], bf),
            pltpu.VMEM((chunks, groups, 2, rows, 2 * HEAD), bf),
            pltpu.VMEM((groups, 2 * total, 2 * rows), bf),
            pltpu.VMEM((groups, total, 2 * rows), bf),
            pltpu.VMEM((chunks, total, 2 * HEAD), f32),
            pltpu.VMEM((chunks, total, 2 * HEAD), f32),
            pltpu.VMEM((chunks, total, 2 * HEAD), f32),
            pltpu.VMEM((chunks, total, 2 * HEAD), bf),
            pltpu.VMEM((chunks, total, 2 * HEAD), bf),
            pltpu.VMEM((slots, tok, HEAD), jnp.int32),
            dma((chunks, 2)), dma((slots,)), dma, dma((chunks,)),
            dma((chunks, groups)), dma((chunks, groups)),
            dma((chunks, groups)), dma((chunks, groups)),
            dma((slots, groups)), dma((slots, groups)),
            dma((chunks,)), dma((chunks,)), dma((chunks,)), dma((chunks,)),
        ],
        compiler_params=pltpu.CompilerParams(
            collective_id=0, has_side_effects=True, vmem_limit_bytes=60 * 1024 * 1024
        ),
    )(tokens, queries, gains, key_weight, value_weight, lengths)


def solution(mesh):
    return jax.shard_map(
        body,
        mesh=mesh,
        in_specs=(
            P("section", None, "fsdp", None),
            P("section", None, "fsdp", None),
            P("section", None),
            P("section", "fsdp", None),
            P("section", "fsdp", None),
            P(),
        ),
        out_specs=P("section", None, "fsdp", None),
        check_vma=False,
    )
```

time: 307 us -> 157 us (0.51)
  waiting for transfers between devices: 243 us -> 0 us
  Pallas kernels: 0 us -> 152 us
  matrix products: 27.5 us -> 0 us
  between operations: 13.6 us -> 0.01 us
  other arithmetic: 11.1 us -> 0 us
  starting transfers between devices: 4.96 us -> 0 us
    all_gather x2 -> x0, waiting for transfers between devices: 234 us -> none  [the longest x1 120 us: body(): lax.all_gather(key_weight[0], 'fsdp', axis=0, tiled=True)]
    pallas_call x0 -> x1, Pallas kernels: none -> 152 us  [body(): pl.pallas_call(functools.partial(kernel, n), out_shape=jax.ShapeDtypeStru...]
    dot_general x4 -> x0, matrix products: 19.3 us -> none  [the longest x2 14 us: add_rows(): return jnp.dot(flat_rows, weight_piece, preferred_element_type=jnp.float32)]
    sub x2 -> x0, matrix products: 8.16 us -> none  [block_attend(): exponent = jnp.where(allowed, jnp.exp(scores - maxima), 0.0)]
    ppermute x2 -> x0, waiting for transfers between devices: 7.35 us -> none  [passed_along(): return lax.ppermute(block, axis, route)]
    ppermute x2 -> x0, starting transfers between devices: 4.92 us -> none  [passed_along(): return lax.ppermute(block, axis, route)]
    convert_element_type x2 -> x0, other arithmetic: 3.9 us -> none  [the longest x1 3.11 us: rms_norm(): (widened * inverse_rms * gain_row.astype(jnp.float32)).astype(jnp.bfloat16)]
    reduce_sum x3 -> x0, other arithmetic: 3.43 us -> none  [the longest x1 3.25 us: rms_norm(): jnp.mean(widened * widened, axis=-1, keepdims=True) + 1e-05]
  transfers between devices with their start and end apart: 4 -> 0, of which waited for: 3 -> 0; matrix products, arithmetic and copies ran while one was open for 9% -> 0% of each run, Pallas kernels for 0% -> 0%
where the time goes in v1:
time: 157 us; the launch traced here: 155 us
  Pallas kernels  152 us (97%)
  local copies, waits for them, and re-layouts  3.13 us (2%)
    pallas_call x1, Pallas kernels, body(): pl.pallas_call(functools.partial(kernel, n), out_shape=jax.ShapeDtypeStru...  152 us

profile of v1, /device:TPU:16, one launch (start us, length us, event | category | flops | bytes accessed | tf_op | source)
XLA Modules:
  0.0 155.1 jit_solution(8390038606026862614)
XLA Ops:
  0.0 152.0 %shard_map.64 = bf16[1,2,128,4096]{3,2,1,0:T(8,128)(2,1)} custom-call(bf16[1,2,128,8192]{3,2,1,0:T(8,128)(2,1)} %x_hbm.1, bf16[1,2,128,4096]{3,2,1,0:T(8,128)(2,1)} %q_hbm.1, bf16[1,8192]{1,0:T(2,128)(2,1)} %gain_ref.1, bf16[1,1024,512]{2,1,0:T(8,128)(2,1)} %kw_hbm.1, bf16[1,1024,512]{2,1,0:T(8,128)(2,1)} %vw_hbm.1, s32[2,16]{1,0:T(2,128)} %len_ref.1), custom_call_target="tpu_custom_call" | custom-call | tf_op jit(solution)/shard_map/pallas_call | solution.py:256
  152.0 3.1 %copy.8 = bf16[1,2,128,4096]{3,2,1,0:T(8,128)(2,1)} copy(bf16[1,2,128,4096]{3,2,1,0:T(8,128)(2,1)} %shard_map.64) | data formatting | bytes 4194304

commit v2 on v1

--- a/solution.py
+++ b/solution.py
@@ -77,6 +77,8 @@
         block = wbuf.at[c, g, side]
         return remote(block, block, ys_sem.at[c, g], yr_sem.at[c, g], y_peer)
 
+    outer = cls == grp % 2
+
     def send_w(c):
         for copy in w_loads[c]:
             copy.wait()
@@ -128,8 +130,10 @@
             return carry
 
         lax.fori_loop(0, tok // block_rows, norm_step, 0)
-        for g in range(groups):
-            x_copy(s, g).start()
+        @pl.when(outer)
+        def _(s=s):
+            for g in range(groups):
+                x_copy(s, g).start()
 
     for c in range(1, chunks):
         send_w(c)
@@ -146,6 +150,15 @@
         start_s[s] = jnp.broadcast_to(start, (tok, HEAD))
     q_load.wait()
 
+    @pl.when(jnp.logical_not(outer))
+    def _():
+        for c in range(chunks):
+            for g in others:
+                w_copy(c, grp, g, dev(g)).wait_send()
+        for s in range(slots):
+            for g in range(groups):
+                x_copy(s, g).start()
+
     def forward(c):
         for g in others:
             w_copy(c, g, g, dev(g)).wait_recv()
@@ -160,16 +173,40 @@
             )
         return acc
 
+    def own_rows(c):
+        own_acc[c] = project(c, 0)
+
+    def y_wait(c):
+        for g in range(groups):
+            y_copy(c, g, 1 - bit).wait_recv()
+
+    @pl.when(outer)
+    def _():
+        for c in range(chunks):
+            forward(c)
+        for c in range(chunks):
+            y_wait(c)
+            own_rows(c)
+
     def stage_a(c):
-        for g in range(groups):
-            y_copy(c, g, 1 - bit).wait_recv()
+        @pl.when(jnp.logical_not(outer))
+        def _():
+            if c == 0:
+                forward(0)
+            if c + 1 < chunks:
+                forward(c + 1)
+            y_wait(c)
+
         if c == 0:
             for s in range(slots):
                 for g in range(groups):
                     x_copy(s, g).wait_recv()
         part_s[c] = project(c, total)
         p_copy(c).start()
-        own_acc[c] = project(c, 0)
+
+        @pl.when(jnp.logical_not(outer))
+        def _():
+            own_rows(c)
 
     def stage_b(c):
         p_copy(c).wait_recv()
@@ -212,23 +249,27 @@
                 o_v[s, :, cols] = mixed.astype(jnp.bfloat16)
                 return carry
 
-            lax.fori_loop(0, q_per_kv, head_step, 0, unroll=2)
+            lax.fori_loop(0, q_per_kv, head_step, 0, unroll=True)
         out_copy(c).start()
 
-    for step in range(chunks + 4):
-        if step < chunks:
-            forward(step)
-        if 1 <= step <= chunks:
-            stage_a(step - 1)
-        if 2 <= step <= chunks + 1:
-            stage_b(step - 2)
-        if 3 <= step <= chunks + 2:
-            stage_c(step - 3)
+    for c in range(chunks - 1):
+        stage_a(c)
+    stage_b(0)
+    stage_b(1)
+    stage_a(chunks - 1)
+    for c in range(2, chunks):
+        stage_c(c - 2)
+        stage_b(c)
+    stage_c(chunks - 2)
+    stage_c(chunks - 1)
 
     for c in range(chunks):
         out_copy(c).wait()
-        for g in others:
-            w_copy(c, grp, g, dev(g)).wait_send()
+        @pl.when(outer)
+        def _(c=c):
+            for g in others:
+                w_copy(c, grp, g, dev(g)).wait_send()
+
         for g in range(groups):
             y_copy(c, g, bit).wait_send()
         p_copy(c).wait_send()

time: 157 us -> 150 us (0.955)
  Pallas kernels: 152 us -> 146 us
    pallas_call x1, Pallas kernels: 152 us -> 146 us  [body(): pl.pallas_call(functools.partial(kernel, n), out_shape=jax.ShapeDtypeStru...]
where the time goes in v2:
time: 150 us
  Pallas kernels  146 us (97%)
  local copies, waits for them, and re-layouts  3.13 us (2%)
    pallas_call x1, Pallas kernels, body(): pl.pallas_call(functools.partial(kernel, n), out_shape=jax.ShapeDtypeStru...  146 us
    unnamed x1, local copies, waits for them, and re-layouts  3.13 us

profile of v2, /device:TPU:16, one launch (start us, length us, event | category | flops | bytes accessed | tf_op | source)
XLA Modules:
  0.0 149.5 jit_solution(2967898657136320626)
XLA Ops:
  0.0 146.4 %shard_map.64 = bf16[1,2,128,4096]{3,2,1,0:T(8,128)(2,1)} custom-call(bf16[1,2,128,8192]{3,2,1,0:T(8,128)(2,1)} %x_hbm.1, bf16[1,2,128,4096]{3,2,1,0:T(8,128)(2,1)} %q_hbm.1, bf16[1,8192]{1,0:T(2,128)(2,1)} %gain_ref.1, bf16[1,1024,512]{2,1,0:T(8,128)(2,1)} %kw_hbm.1, bf16[1,1024,512]{2,1,0:T(8,128)(2,1)} %vw_hbm.1, s32[2,16]{1,0:T(2,128)} %len_ref.1), custom_call_target="tpu_custom_call" | custom-call | tf_op jit(solution)/shard_map/pallas_call | solution.py:297
  146.4 3.1 %copy.8 = bf16[1,2,128,4096]{3,2,1,0:T(8,128)(2,1)} copy(bf16[1,2,128,4096]{3,2,1,0:T(8,128)(2,1)} %shard_map.64) | data formatting | bytes 4194304

commit v3 on v2

--- a/solution.py
+++ b/solution.py
@@ -14,7 +14,7 @@
 def kernel(
     n,
     x_hbm, q_hbm, gain_ref, kw_hbm, vw_hbm, len_ref, o_hbm,
-    x_v, q_v, o_v, wbuf, xs, sx, part_s, part_r, own_acc, kv, prior, start_s,
+    x_v, q_v, o_v, wbuf, xs, sx, pk_s, pk_r, pv_s, pv_r, own_acc, kv, prior, start_s,
     lw_sem, lx_sem, lq_sem, lo_sem,
     ws_sem, wr_sem, ys_sem, yr_sem, xs_sem, xr_sem, ps_sem, pr_sem, ks_sem, kr_sem,
 ):
@@ -92,13 +92,18 @@
             xs_sem.at[s, g], xr_sem.at[s, g], z_peer,
         )
 
-    def p_copy(c):
-        return remote(part_s.at[c], part_r.at[c], ps_sem.at[c], pr_sem.at[c], z_peer)
+    def p_copies(c):
+        return [
+            remote(src.at[c], dst.at[c], ps_sem.at[c, i], pr_sem.at[c, i], z_peer)
+            for i, (src, dst) in enumerate(((pk_s, pk_r), (pv_s, pv_r)))
+        ]
 
     def k_copy(c):
         return remote(kv.at[c], prior.at[c], ks_sem.at[c], kr_sem.at[c], right)
 
-    send_w(0)
+    @pl.when(jnp.logical_not(outer))
+    def _():
+        send_w(0)
 
     block_rows = 16
 
@@ -134,6 +139,10 @@
         def _(s=s):
             for g in range(groups):
                 x_copy(s, g).start()
+
+    @pl.when(outer)
+    def _():
+        send_w(0)
 
     for c in range(1, chunks):
         send_w(c)
@@ -201,16 +210,21 @@
             for s in range(slots):
                 for g in range(groups):
                     x_copy(s, g).wait_recv()
-        part_s[c] = project(c, total)
-        p_copy(c).start()
+        partial = project(c, total)
+        pk_s[c] = partial[:, :HEAD]
+        pv_s[c] = partial[:, HEAD:].astype(jnp.bfloat16)
+        for copy in p_copies(c):
+            copy.start()
 
         @pl.when(jnp.logical_not(outer))
         def _():
             own_rows(c)
 
     def stage_b(c):
-        p_copy(c).wait_recv()
-        kv[c] = (own_acc[c] + part_r[c]).astype(jnp.bfloat16)
+        for copy in p_copies(c):
+            copy.wait_recv()
+        kv[c, :, 0:HEAD] = (own_acc[c, :, 0:HEAD] + pk_r[c]).astype(jnp.bfloat16)
+        kv[c, :, HEAD:] = (own_acc[c, :, HEAD:] + pv_r[c].astype(jnp.float32)).astype(jnp.bfloat16)
 
         @pl.when(me < n - 1)
         def _():
@@ -272,7 +286,8 @@
 
         for g in range(groups):
             y_copy(c, g, bit).wait_send()
-        p_copy(c).wait_send()
+        for copy in p_copies(c):
+            copy.wait_send()
 
         @pl.when(me < n - 1)
         def _(c=c):
@@ -306,8 +321,10 @@
             pltpu.VMEM((chunks, groups, 2, rows, 2 * HEAD), bf),
             pltpu.VMEM((groups, 2 * total, 2 * rows), bf),
             pltpu.VMEM((groups, total, 2 * rows), bf),
-            pltpu.VMEM((chunks, total, 2 * HEAD), f32),
-            pltpu.VMEM((chunks, total, 2 * HEAD), f32),
+            pltpu.VMEM((chunks, total, HEAD), f32),
+            pltpu.VMEM((chunks, total, HEAD), f32),
+            pltpu.VMEM((chunks, total, HEAD), bf),
+            pltpu.VMEM((chunks, total, HEAD), bf),
             pltpu.VMEM((chunks, total, 2 * HEAD), f32),
             pltpu.VMEM((chunks, total, 2 * HEAD), bf),
             pltpu.VMEM((chunks, total, 2 * HEAD), bf),
@@ -316,7 +333,7 @@
             dma((chunks, groups)), dma((chunks, groups)),
             dma((chunks, groups)), dma((chunks, groups)),
             dma((slots, groups)), dma((slots, groups)),
-            dma((chunks,)), dma((chunks,)), dma((chunks,)), dma((chunks,)),
+            dma((chunks, 2)), dma((chunks, 2)), dma((chunks,)), dma((chunks,)),
         ],
         compiler_params=pltpu.CompilerParams(
             collective_id=0, has_side_effects=True, vmem_limit_bytes=60 * 1024 * 1024

time: 150 us -> 137 us (0.913)
  Pallas kernels: 146 us -> 133 us
    pallas_call x1, Pallas kernels: 146 us -> 133 us  [body(): pl.pallas_call(functools.partial(kernel, n), out_shape=jax.ShapeDtypeStru...]
where the time goes in v3:
time: 137 us; the launch traced here: 136 us
  Pallas kernels  133 us (97%)
  local copies, waits for them, and re-layouts  3.13 us (2%)
    pallas_call x1, Pallas kernels, body(): pl.pallas_call(functools.partial(kernel, n), out_shape=jax.ShapeDtypeStru...  133 us
    unnamed x1, local copies, waits for them, and re-layouts  3.13 us

profile of v3, /device:TPU:16, one launch (start us, length us, event | category | flops | bytes accessed | tf_op | source)
XLA Modules:
  0.0 135.8 jit_solution(15436604346113700235)
XLA Ops:
  0.0 132.7 %shard_map.64 = bf16[1,2,128,4096]{3,2,1,0:T(8,128)(2,1)} custom-call(bf16[1,2,128,8192]{3,2,1,0:T(8,128)(2,1)} %x_hbm.1, bf16[1,2,128,4096]{3,2,1,0:T(8,128)(2,1)} %q_hbm.1, bf16[1,8192]{1,0:T(2,128)(2,1)} %gain_ref.1, bf16[1,1024,512]{2,1,0:T(8,128)(2,1)} %kw_hbm.1, bf16[1,1024,512]{2,1,0:T(8,128)(2,1)} %vw_hbm.1, s32[2,16]{1,0:T(2,128)} %len_ref.1), custom_call_target="tpu_custom_call" | custom-call | tf_op jit(solution)/shard_map/pallas_call | solution.py:312
  132.7 3.1 %copy.8 = bf16[1,2,128,4096]{3,2,1,0:T(8,128)(2,1)} copy(bf16[1,2,128,4096]{3,2,1,0:T(8,128)(2,1)} %shard_map.64) | data formatting | bytes 4194304
